TPU v7x, 32 devices: a whole 2x2x4 slice. The times are simulated.
32 devices in a mesh: row: 8 (over z, y), col: 4 (over x, core).
Axes of the slice: x: 2, y: 2, z: 4, core: 2. Of those that a mesh axis runs over, the one named last changes fastest.
Arguments:
- q_start: bfloat16 [8192, 32], P(('row', 'col')), may hold values from -6 to 6
- row_scale: float32 [8192], P(('row', 'col')), may hold values from 0.25 to 4
- near_blocks: bfloat16 [8, 128, 256, 256], P('row', 'col'), may hold values from -0.0625 to 0.0625
- near_rows: int32 [8, 4, 32], P('row', 'col'), may hold values from 0 to 3
- near_cols: int32 [8, 4, 32], P('row', 'col'), may hold values from 0 to 7
- far_ut: bfloat16 [8, 512, 32, 256], P('row', 'col'), may hold values from -0.1875 to 0.1875
- far_vt: bfloat16 [8, 512, 32, 256], P('row', 'col'), may hold values from -0.375 to 0.375
- far_rank: int32 [8, 4, 128], P('row', 'col'), may hold values from 8 to 32, as said below
- far_rows: int32 [8, 4, 128], P('row', 'col'), may hold values from 0 to 3
- far_cols: int32 [8, 4, 128], P('row', 'col'), may hold values from 0 to 7
Outputs:
- basis: float32 [8192, 32], P(('row', 'col'))
- factor: float32 [32, 32], replicated
Inputs may be any that keep to these rules, and one draw needn't show every extreme that they name: `far_rank`: each device has a far block of rank 32.
All inputs are finite; a program needn't handle non-finite values.
Results may differ from a plain program's by a relative error of at most 0.016.
Values may be sent and summed in bfloat16 or wider, within the bound.
A program may use at most 128 MiB of HBM per device.

v0:
```python
import functools

import jax
import jax.numpy as jnp
from jax import lax
from jax.experimental import pallas as pl
from jax.experimental.pallas import tpu as pltpu
from jax.sharding import PartitionSpec as P

ITERS = 4
MESH = pl.DeviceIdType.MESH
HIGH = lax.Precision.HIGHEST
NT = (((1,), (1,)), ((), ()))
LANES = 128
SUB = 8
TILE = 256


def dot_nt(a, b, precision=None):
    return lax.dot_general(a, b, NT, precision=precision, preferred_element_type=jnp.float32)


def partner(index, step, size):
    if size & (size - 1):
        return lax.rem(index + step, size)
    out, bit = 0, 1
    while bit < size:
        mine = (index // bit) % 2
        out = out + bit * (1 - mine if step & bit else mine)
        bit *= 2
    return out


def factorize(work, kcols):
    blocks = kcols // SUB
    w = [work[SUB * q : SUB * (q + 1), :] for q in range(blocks)]
    sub = lax.broadcasted_iota(jnp.int32, (SUB, LANES), 0)
    diag = []
    for p in range(blocks):
        cb = [
            [
                jnp.broadcast_to(w[q][:, kcols + SUB * p + j : kcols + SUB * p + j + 1], (SUB, LANES))
                if q >= p
                else None
                for q in range(blocks)
            ]
            for j in range(SUB)
        ]
        dp = jnp.ones((SUB, LANES), jnp.float32)
        for j in range(SUB):
            d = jnp.broadcast_to(cb[j][p][j : j + 1, :], (SUB, LANES))
            dp = jnp.where(sub == j, d, dp)
            inv = 1.0 / d
            row = jnp.broadcast_to(w[p][j : j + 1, :], (SUB, LANES)) * inv
            others = {
                k: jnp.broadcast_to(cb[k][p][j : j + 1, :], (SUB, LANES)) * inv
                for k in range(j + 1, SUB)
            }
            for q in range(p, blocks):
                m = cb[j][q]
                if q == p:
                    m = jnp.where(sub > j, m, 0.0)
                w[q] = w[q] - m * row
                for k in range(j + 1, SUB):
                    cb[k][q] = cb[k][q] - m * others[k]
        diag.append(dp)
    return jnp.concatenate([w[q] * lax.rsqrt(diag[q]) for q in range(blocks)], axis=0)


def apply_inverse(rows, product):
    pad = jnp.zeros((LANES - product.shape[0], product.shape[1]), jnp.float32)
    return jnp.dot(
        rows,
        jnp.concatenate([product, pad], axis=0),
        precision=HIGH,
        preferred_element_type=jnp.float32,
    )


def finish(rows_ref, prod_ref, basis_ref, factor_ref):
    rows = rows_ref[...]
    kcols = rows.shape[0]
    lane = lax.broadcasted_iota(jnp.int32, rows.shape, 1)
    sub = lax.broadcasted_iota(jnp.int32, rows.shape, 0)
    basis_ref[...] = apply_inverse(rows, prod_ref[...])
    upper = jnp.where(lane - kcols >= sub, rows, 0.0)
    pick = jnp.where(lane == sub + kcols, 1.0, 0.0).astype(jnp.float32)
    factor_ref[...] = dot_nt(pick, upper, HIGH)


def kernel(
    n_row,
    n_col,
    total_pts,
    q_ref,
    scale_ref,
    rank_ref,
    fr_ref,
    fc_ref,
    nr_ref,
    nc_ref,
    near_hbm,
    ut_hbm,
    vt_hbm,
    rows_ref,
    prod_ref,
    near_ref,
    ut_ref,
    vt_ref,
    ag_refs,
    sel_ref,
    lhs_ref,
    part_ref,
    out_ref,
    rs_ref,
    ga_ref,
    gb_ref,
    load_sem,
    ag_send,
    ag_recv,
    rs_send,
    rs_recv,
    ga_send,
    ga_recv,
    gb_send,
    gb_recv,
):
    row = lax.axis_index("row")
    col = lax.axis_index("col")
    kcols, leaf = q_ref.shape
    groups = LANES // kcols
    far_tiles = ut_ref.shape[0] // TILE
    n_near = near_ref.shape[0]
    rank_max = ut_ref.shape[0] // rank_ref.shape[0]

    loads = [
        pltpu.make_async_copy(src, dst, load_sem.at[i])
        for i, (src, dst) in enumerate(((vt_hbm, vt_ref), (ut_hbm, ut_ref), (near_hbm, near_ref)))
    ]
    for copy in loads:
        copy.start()

    def ag_copy(t, peer):
        return pltpu.make_async_remote_copy(
            src_ref=ag_refs[t].at[row],
            dst_ref=ag_refs[t].at[row],
            send_sem=ag_send.at[t],
            recv_sem=ag_recv.at[t],
            device_id=(peer, col),
            device_id_type=MESH,
        )

    def gather_start(t, value):
        ag_refs[t][row] = value
        for d in range(n_row - 1, 0, -1):
            ag_copy(t, partner(row, d, n_row)).start()

    def wait_like(view, sem):
        pltpu.make_async_copy(view, view, sem).wait()

    def gather_wait(t):
        view = ag_refs[t].at[pl.ds(0, n_row - 1)]
        wait_like(view, ag_send.at[t])
        wait_like(view, ag_recv.at[t])

    def scatter_start(t):
        for d in range(n_col - 1, 0, -1):
            peer = lax.rem(col + d, n_col)
            pltpu.make_async_remote_copy(
                src_ref=out_ref.at[t, peer],
                dst_ref=rs_ref.at[t, d - 1],
                send_sem=rs_send.at[t],
                recv_sem=rs_recv.at[t],
                device_id=(row, peer),
                device_id_type=MESH,
            ).start()

    def scatter_wait(t):
        view = rs_ref.at[t]
        wait_like(view, rs_send.at[t])
        wait_like(view, rs_recv.at[t])

    def gram_col_start(t, value):
        ga_ref[t, col] = value
        for d in range(1, n_col):
            pltpu.make_async_remote_copy(
                src_ref=ga_ref.at[t, col],
                dst_ref=ga_ref.at[t, col],
                send_sem=ga_send.at[t],
                recv_sem=ga_recv.at[t],
                device_id=(row, lax.rem(col + d, n_col)),
                device_id_type=MESH,
            ).start()

    def gram_row_start(t):
        view = ga_ref.at[t, pl.ds(0, n_col - 1)]
        wait_like(view, ga_send.at[t])
        wait_like(view, ga_recv.at[t])
        gb_ref[t, row] = jnp.sum(ga_ref[t], axis=0)
        for d in range(n_row - 1, 0, -1):
            pltpu.make_async_remote_copy(
                src_ref=gb_ref.at[t, row],
                dst_ref=gb_ref.at[t, row],
                send_sem=gb_send.at[t],
                recv_sem=gb_recv.at[t],
                device_id=(partner(row, d, n_row), col),
                device_id_type=MESH,
            ).start()

    def gram_wait(t):
        view = gb_ref.at[t, pl.ds(0, n_row - 1)]
        wait_like(view, gb_send.at[t])
        wait_like(view, gb_recv.at[t])

    def selectors():
        place = lax.broadcasted_iota(jnp.int32, (SUB, TILE), 1)
        owner, rank_of = place // rank_max, lax.rem(place, rank_max)

        def tile(i, carry):
            fc = jnp.zeros((SUB, TILE), jnp.int32)
            fr, keep = fc, fc
            for j in range(TILE // rank_max):
                b = i * (TILE // rank_max) + j
                fc = jnp.where(owner == j, fc_ref[b], fc)
                fr = jnp.where(owner == j, fr_ref[b], fr)
                keep = jnp.where(owner == j, rank_ref[b], keep)
            start = pl.multiple_of(i * TILE, TILE)
            sel_ref[0, :, pl.ds(start, TILE)] = jnp.where(rank_of < keep, fc, -1)
            sel_ref[1, :, pl.ds(start, TILE)] = fr
            return carry

        lax.fori_loop(0, far_tiles, tile, 0)

    def operator(t, first):
        if first:
            loads[0].wait()
        q_all = ag_refs[t][...].reshape(n_row * kcols, leaf)

        def far_tile(i, carry):
            start = pl.multiple_of(i * TILE, TILE)
            y = dot_nt(q_all, vt_ref[pl.ds(start, TILE), :])
            fc = jnp.concatenate([sel_ref[0, :, pl.ds(start, TILE)]] * (kcols // SUB), axis=0)
            fr = jnp.concatenate([sel_ref[1, :, pl.ds(start, TILE)]] * (kcols // SUB), axis=0)
            inner = jnp.zeros((kcols, TILE), jnp.float32)
            for c in range(n_row):
                inner = jnp.where(fc == c, y[c * kcols : (c + 1) * kcols, :], inner)
            for r in range(n_col):
                lhs_ref[r * kcols : (r + 1) * kcols, pl.ds(start, TILE)] = jnp.where(
                    fr == r, inner, 0.0
                ).astype(jnp.bfloat16)
            return carry

        lax.fori_loop(0, far_tiles, far_tile, 0, unroll=True)
        if first:
            loads[1].wait()
        far = jnp.dot(lhs_ref[...], ut_ref[...], preferred_element_type=jnp.float32)
        for r in range(n_col):
            part_ref[t, r] = far[r * kcols : (r + 1) * kcols, :]
        if first:
            loads[2].wait()

        def near_block(b, acc):
            z = dot_nt(ag_refs[t][nc_ref[b]], near_ref[b])
            r_of = nr_ref[b]
            return tuple(
                a + z * jnp.where(r_of == r, 1.0, 0.0).astype(jnp.float32) for r, a in enumerate(acc)
            )

        zero = jnp.zeros((kcols, leaf), jnp.float32)
        near = lax.fori_loop(0, n_near, near_block, (zero,) * n_col, unroll=True)
        for r in range(n_col):
            whole = part_ref[t, r] + near[r]
            part_ref[t, r] = whole
            out_ref[t, r] = whole.astype(jnp.bfloat16)

    lane = lax.broadcasted_iota(jnp.int32, (SUB, LANES), 1)
    lane_full = lax.broadcasted_iota(jnp.int32, (kcols, LANES), 1)
    sub_full = lax.broadcasted_iota(jnp.int32, (kcols, LANES), 0)

    def pack_gram(product):
        tiled = jnp.concatenate([product] * groups, axis=0)
        g = dot_nt(product, tiled, HIGH)
        rows = kcols // groups
        packed = jnp.zeros((rows, LANES), jnp.float32)
        for i in range(groups):
            packed = jnp.where(lane // kcols == i, g[i * rows : (i + 1) * rows, :], packed)
        return packed

    def solve(t):
        g = jnp.sum(gb_ref[t], axis=0) / total_pts
        parts = []
        for i in range(groups):
            shift = (1 - i) * kcols % LANES
            parts.append(pltpu.roll(g, shift, 1) if shift else g)
        s = jnp.concatenate(parts, axis=0)
        work = jnp.where(lane_full < kcols, jnp.where(lane_full == sub_full, 1.0, 0.0), s)
        work = jnp.where(lane_full < 2 * kcols, work, 0.0)
        return factorize(work, kcols)

    gather_start(0, q_ref[...])
    selectors()
    for t in range(ITERS):
        if t > 0:
            gram_row_start(t - 1)
        gather_wait(t)
        operator(t, t == 0)
        scatter_start(t)
        if t > 0:
            gram_wait(t - 1)
            rows = solve(t - 1)
        scatter_wait(t)
        total = part_ref[t, col]
        for d in range(1, n_col):
            total = total + rs_ref[t, d - 1].astype(jnp.float32)
        product = total * scale_ref[...]
        if t > 0:
            product = apply_inverse(rows, product)
        if t < ITERS - 1:
            gather_start(t + 1, product.astype(jnp.bfloat16))
        gram_col_start(t, pack_gram(product))
    prod_ref[...] = product
    gram_row_start(ITERS - 1)
    gram_wait(ITERS - 1)
    rows_ref[...] = solve(ITERS - 1)


def on_device(
    q_start,
    row_scale,
    near_blocks,
    near_rows,
    near_cols,
    far_ut,
    far_vt,
    far_rank,
    far_rows,
    far_cols,
):
    leaf, kcols = q_start.shape
    n_row = lax.axis_size("row")
    n_col = lax.axis_size("col")
    n_dev = n_row * n_col
    n_near = near_blocks.shape[1]
    n_far, rank_max = far_ut.shape[1:3]
    near = near_blocks[0]
    ut = far_ut.reshape(n_far * rank_max, leaf)
    vt = far_vt.reshape(n_far * rank_max, leaf)
    vmem = pl.BlockSpec(memory_space=pltpu.VMEM)
    smem = pl.BlockSpec(memory_space=pltpu.SMEM)
    hbm = pl.BlockSpec(memory_space=pl.ANY)
    f32, bf16 = jnp.float32, jnp.bfloat16
    rows, product = pl.pallas_call(
        functools.partial(kernel, n_row, n_col, leaf * n_dev),
        name="subspace",
        out_shape=(
            jax.ShapeDtypeStruct((kcols, LANES), f32),
            jax.ShapeDtypeStruct((kcols, leaf), f32),
        ),
        in_specs=[vmem, vmem, smem, smem, smem, smem, smem, hbm, hbm, hbm],
        out_specs=(vmem, vmem),
        scratch_shapes=[
            pltpu.VMEM(near.shape, bf16),
            pltpu.VMEM(ut.shape, bf16),
            pltpu.VMEM(vt.shape, bf16),
            [pltpu.VMEM((n_row, kcols, leaf), bf16) for _ in range(ITERS)],
            pltpu.VMEM((2, SUB, n_far * rank_max), jnp.int32),
            pltpu.VMEM((n_col * kcols, n_far * rank_max), bf16),
            pltpu.VMEM((ITERS, n_col, kcols, leaf), f32),
            pltpu.VMEM((ITERS, n_col, kcols, leaf), bf16),
            pltpu.VMEM((ITERS, n_col - 1, kcols, leaf), bf16),
            pltpu.VMEM((ITERS, n_col, kcols * kcols // LANES, LANES), f32),
            pltpu.VMEM((ITERS, n_row, kcols * kcols // LANES, LANES), f32),
            pltpu.SemaphoreType.DMA((3,)),
            pltpu.SemaphoreType.DMA((ITERS,)),
            pltpu.SemaphoreType.DMA((ITERS,)),
            pltpu.SemaphoreType.DMA((ITERS,)),
            pltpu.SemaphoreType.DMA((ITERS,)),
            pltpu.SemaphoreType.DMA((ITERS,)),
            pltpu.SemaphoreType.DMA((ITERS,)),
            pltpu.SemaphoreType.DMA((ITERS,)),
            pltpu.SemaphoreType.DMA((ITERS,)),
        ],
        compiler_params=pltpu.CompilerParams(
            has_side_effects=True, vmem_limit_bytes=56 * 1024 * 1024
        ),
    )(
        q_start.T,
        row_scale.reshape(1, leaf),
        far_rank[0, 0],
        far_rows[0, 0],
        far_cols[0, 0],
        near_rows[0, 0],
        near_cols[0, 0],
        near,
        ut,
        vt,
    )
    basis_t, factor = pl.pallas_call(
        finish,
        name="finish",
        out_shape=(
            jax.ShapeDtypeStruct((kcols, leaf), f32),
            jax.ShapeDtypeStruct((kcols, kcols), f32),
        ),
        in_specs=[vmem, vmem],
        out_specs=(vmem, vmem),
    )(rows, product)
    return basis_t.T, factor


def solution(mesh):
    in_specs = (
        P(("row", "col"), None),
        P(("row", "col")),
        P("row", "col", None, None),
        P("row", "col", None),
        P("row", "col", None),
        P("row", "col", None, None),
        P("row", "col", None, None),
        P("row", "col", None),
        P("row", "col", None),
        P("row", "col", None),
    )
    out_specs = (P(("row", "col"), None), P())
    return jax.shard_map(
        on_device, mesh=mesh, in_specs=in_specs, out_specs=out_specs, check_vma=False
    )
```

profile of v0, /device:TPU:0, one launch (start us, length us, event | category | flops | bytes accessed | tf_op | source)
XLA Modules:
  0.0 62.3 jit_solution(3716578561610379005)
XLA Ops:
  0.6 60.1 %subspace.1 = (f32[32,128]{1,0:T(8,128)}, f32[32,256]{1,0:T(8,128)}) custom-call(bf16[32,256]{1,0:T(8,128)(2,1)} %bitcast.14, f32[1,256]{1,0:T(1,128)} %bitcast.15, s32[128]{0:T(128)} %bitcast.16, s32[128]{0:T(128)} %bitcast.17, s32[128]{0:T(128)} %bitcast.18, s32[32]{0:T(128)} %bitcast.19, s32[32]{0:T(128)} %bitcast.20, bf16[32,256,256]{2,1,0:T(8,128)(2,1)} %bitcast.11, ...), custom_call_target="tpu_custom_call" | custom-call | tf_op jit(solution)/shard_map/subspace/pallas_call | solution.py:352
  60.7 1.6 %finish.1 = (f32[32,256]{1,0:T(8,128)}, f32[32,32]{1,0:T(8,128)}) custom-call(f32[32,128]{1,0:T(8,128)} %get-tuple-element.6.rows_ref, f32[32,256]{1,0:T(8,128)} %get-tuple-element.7.prod_ref), custom_call_target="tpu_custom_call" | custom-call | tf_op jit(solution)/shard_map/finish/pallas_call | solution.py:398
where the time goes:
time: 62.6 us; the launch traced here: 62.3 us
  Pallas kernels  61.7 us (99%)
  between operations  0.64 us (1%)
    pallas_call x1, Pallas kernels, on_device(): pl.pallas_call(functools.partial(kernel, n_row, n_col, leaf * n_dev), nam...  60.1 us
    pallas_call x1, Pallas kernels, on_device(): pl.pallas_call(finish, name='finish', out_shape=(jax.ShapeDtypeStruct((kc...  1.58 us

commit v1 on v0

--- a/solution.py
+++ b/solution.py
@@ -92,18 +92,24 @@
     n_row,
     n_col,
     total_pts,
-    q_ref,
+    q_hbm,
+    scale_hbm,
+    rank_hbm,
+    fr_hbm,
+    fc_hbm,
+    nr_hbm,
+    nc_hbm,
+    near_hbm,
+    ut_hbm,
+    vt_hbm,
+    rows_ref,
+    prod_ref,
     scale_ref,
     rank_ref,
     fr_ref,
     fc_ref,
     nr_ref,
     nc_ref,
-    near_hbm,
-    ut_hbm,
-    vt_hbm,
-    rows_ref,
-    prod_ref,
     near_ref,
     ut_ref,
     vt_ref,
@@ -127,15 +133,37 @@
 ):
     row = lax.axis_index("row")
     col = lax.axis_index("col")
-    kcols, leaf = q_ref.shape
+    kcols, leaf = q_hbm.shape
     groups = LANES // kcols
     far_tiles = ut_ref.shape[0] // TILE
     n_near = near_ref.shape[0]
     rank_max = ut_ref.shape[0] // rank_ref.shape[0]
 
+    pair = 2 if n_row % 2 == 0 else 1
+    low, high = lax.rem(row, pair), row // pair
+    n_low, n_high = n_col * pair, n_row // pair
+    peers = [(partner(row, d, n_row), col) for d in range(1, n_row)]
+    for e in range(pair):
+        for d in range(1, n_col):
+            peers.append((high * pair + lax.rem(low + e, pair), lax.rem(col + d, n_col)))
+    barrier = pltpu.get_barrier_semaphore()
+    for peer in peers:
+        pl.semaphore_signal(barrier, inc=1, device_id=peer, device_id_type=MESH)
+
+    moves = (
+        (q_hbm, ag_refs[0].at[row]),
+        (rank_hbm, rank_ref),
+        (fr_hbm, fr_ref),
+        (fc_hbm, fc_ref),
+        (vt_hbm, vt_ref),
+        (ut_hbm, ut_ref),
+        (nr_hbm, nr_ref),
+        (nc_hbm, nc_ref),
+        (scale_hbm, scale_ref),
+        (near_hbm, near_ref),
+    )
     loads = [
-        pltpu.make_async_copy(src, dst, load_sem.at[i])
-        for i, (src, dst) in enumerate(((vt_hbm, vt_ref), (ut_hbm, ut_ref), (near_hbm, near_ref)))
+        pltpu.make_async_copy(src, dst, load_sem.at[i]) for i, (src, dst) in enumerate(moves)
     ]
     for copy in loads:
         copy.start()
@@ -150,8 +178,7 @@
             device_id_type=MESH,
         )
 
-    def gather_start(t, value):
-        ag_refs[t][row] = value
+    def gather_start(t):
         for d in range(n_row - 1, 0, -1):
             ag_copy(t, partner(row, d, n_row)).start()
 
@@ -180,35 +207,42 @@
         wait_like(view, rs_send.at[t])
         wait_like(view, rs_recv.at[t])
 
-    def gram_col_start(t, value):
-        ga_ref[t, col] = value
-        for d in range(1, n_col):
+    def gram_low_start(t, value):
+        mine = low * n_col + col
+        ga_ref[t, mine] = value
+        for e in range(pair - 1, -1, -1):
+            for d in range(n_col - 1, -1, -1):
+                if (d, e) == (0, 0):
+                    continue
+                pltpu.make_async_remote_copy(
+                    src_ref=ga_ref.at[t, mine],
+                    dst_ref=ga_ref.at[t, mine],
+                    send_sem=ga_send.at[t],
+                    recv_sem=ga_recv.at[t],
+                    device_id=(
+                        high * pair + lax.rem(low + e, pair),
+                        lax.rem(col + d, n_col),
+                    ),
+                    device_id_type=MESH,
+                ).start()
+
+    def gram_high_start(t):
+        view = ga_ref.at[t, pl.ds(0, n_low - 1)]
+        wait_like(view, ga_send.at[t])
+        wait_like(view, ga_recv.at[t])
+        gb_ref[t, high] = jnp.sum(ga_ref[t], axis=0)
+        for d in range(n_high - 1, 0, -1):
             pltpu.make_async_remote_copy(
-                src_ref=ga_ref.at[t, col],
-                dst_ref=ga_ref.at[t, col],
-                send_sem=ga_send.at[t],
-                recv_sem=ga_recv.at[t],
-                device_id=(row, lax.rem(col + d, n_col)),
+                src_ref=gb_ref.at[t, high],
+                dst_ref=gb_ref.at[t, high],
+                send_sem=gb_send.at[t],
+                recv_sem=gb_recv.at[t],
+                device_id=(partner(high, d, n_high) * pair + low, col),
                 device_id_type=MESH,
             ).start()
 
-    def gram_row_start(t):
-        view = ga_ref.at[t, pl.ds(0, n_col - 1)]
-        wait_like(view, ga_send.at[t])
-        wait_like(view, ga_recv.at[t])
-        gb_ref[t, row] = jnp.sum(ga_ref[t], axis=0)
-        for d in range(n_row - 1, 0, -1):
-            pltpu.make_async_remote_copy(
-                src_ref=gb_ref.at[t, row],
-                dst_ref=gb_ref.at[t, row],
-                send_sem=gb_send.at[t],
-                recv_sem=gb_recv.at[t],
-                device_id=(partner(row, d, n_row), col),
-                device_id_type=MESH,
-            ).start()
-
     def gram_wait(t):
-        view = gb_ref.at[t, pl.ds(0, n_row - 1)]
+        view = gb_ref.at[t, pl.ds(0, n_high - 1)]
         wait_like(view, gb_send.at[t])
         wait_like(view, gb_recv.at[t])
 
@@ -233,7 +267,7 @@
 
     def operator(t, first):
         if first:
-            loads[0].wait()
+            loads[4].wait()
         q_all = ag_refs[t][...].reshape(n_row * kcols, leaf)
 
         def far_tile(i, carry):
@@ -252,12 +286,13 @@
 
         lax.fori_loop(0, far_tiles, far_tile, 0, unroll=True)
         if first:
-            loads[1].wait()
+            loads[5].wait()
         far = jnp.dot(lhs_ref[...], ut_ref[...], preferred_element_type=jnp.float32)
         for r in range(n_col):
             part_ref[t, r] = far[r * kcols : (r + 1) * kcols, :]
         if first:
-            loads[2].wait()
+            for i in (6, 7, 9):
+                loads[i].wait()
 
         def near_block(b, acc):
             z = dot_nt(ag_refs[t][nc_ref[b]], near_ref[b])
@@ -297,17 +332,23 @@
         work = jnp.where(lane_full < 2 * kcols, work, 0.0)
         return factorize(work, kcols)
 
-    gather_start(0, q_ref[...])
+    for i in (1, 2, 3):
+        loads[i].wait()
     selectors()
+    loads[0].wait()
+    pl.semaphore_wait(barrier, len(peers))
+    gather_start(0)
     for t in range(ITERS):
         if t > 0:
-            gram_row_start(t - 1)
+            gram_high_start(t - 1)
         gather_wait(t)
         operator(t, t == 0)
         scatter_start(t)
         if t > 0:
             gram_wait(t - 1)
             rows = solve(t - 1)
+        if t == 0:
+            loads[8].wait()
         scatter_wait(t)
         total = part_ref[t, col]
         for d in range(1, n_col):
@@ -316,10 +357,11 @@
         if t > 0:
             product = apply_inverse(rows, product)
         if t < ITERS - 1:
-            gather_start(t + 1, product.astype(jnp.bfloat16))
-        gram_col_start(t, pack_gram(product))
+            ag_refs[t + 1][row] = product.astype(jnp.bfloat16)
+            gather_start(t + 1)
+        gram_low_start(t, pack_gram(product))
     prod_ref[...] = product
-    gram_row_start(ITERS - 1)
+    gram_high_start(ITERS - 1)
     gram_wait(ITERS - 1)
     rows_ref[...] = solve(ITERS - 1)
 
@@ -340,25 +382,32 @@
     n_row = lax.axis_size("row")
     n_col = lax.axis_size("col")
     n_dev = n_row * n_col
+    pair = 2 if n_row % 2 == 0 else 1
+    n_low, n_high = n_col * pair, n_row // pair
     n_near = near_blocks.shape[1]
     n_far, rank_max = far_ut.shape[1:3]
     near = near_blocks[0]
     ut = far_ut.reshape(n_far * rank_max, leaf)
     vt = far_vt.reshape(n_far * rank_max, leaf)
     vmem = pl.BlockSpec(memory_space=pltpu.VMEM)
-    smem = pl.BlockSpec(memory_space=pltpu.SMEM)
     hbm = pl.BlockSpec(memory_space=pl.ANY)
     f32, bf16 = jnp.float32, jnp.bfloat16
     rows, product = pl.pallas_call(
         functools.partial(kernel, n_row, n_col, leaf * n_dev),
         name="subspace",
         out_shape=(
-            jax.ShapeDtypeStruct((kcols, LANES), f32),
-            jax.ShapeDtypeStruct((kcols, leaf), f32),
+            pltpu.VMEM((kcols, LANES), f32),
+            pltpu.VMEM((kcols, leaf), f32),
         ),
-        in_specs=[vmem, vmem, smem, smem, smem, smem, smem, hbm, hbm, hbm],
+        in_specs=[hbm] * 10,
         out_specs=(vmem, vmem),
         scratch_shapes=[
+            pltpu.VMEM((1, leaf), f32),
+            pltpu.SMEM((n_far,), jnp.int32),
+            pltpu.SMEM((n_far,), jnp.int32),
+            pltpu.SMEM((n_far,), jnp.int32),
+            pltpu.SMEM((n_near,), jnp.int32),
+            pltpu.SMEM((n_near,), jnp.int32),
             pltpu.VMEM(near.shape, bf16),
             pltpu.VMEM(ut.shape, bf16),
             pltpu.VMEM(vt.shape, bf16),
@@ -368,9 +417,9 @@
             pltpu.VMEM((ITERS, n_col, kcols, leaf), f32),
             pltpu.VMEM((ITERS, n_col, kcols, leaf), bf16),
             pltpu.VMEM((ITERS, n_col - 1, kcols, leaf), bf16),
-            pltpu.VMEM((ITERS, n_col, kcols * kcols // LANES, LANES), f32),
-            pltpu.VMEM((ITERS, n_row, kcols * kcols // LANES, LANES), f32),
-            pltpu.SemaphoreType.DMA((3,)),
+            pltpu.VMEM((ITERS, n_low, kcols * kcols // LANES, LANES), f32),
+            pltpu.VMEM((ITERS, n_high, kcols * kcols // LANES, LANES), f32),
+            pltpu.SemaphoreType.DMA((10,)),
             pltpu.SemaphoreType.DMA((ITERS,)),
             pltpu.SemaphoreType.DMA((ITERS,)),
             pltpu.SemaphoreType.DMA((ITERS,)),
@@ -381,7 +430,7 @@
             pltpu.SemaphoreType.DMA((ITERS,)),
         ],
         compiler_params=pltpu.CompilerParams(
-            has_side_effects=True, vmem_limit_bytes=56 * 1024 * 1024
+            collective_id=0, has_side_effects=True, vmem_limit_bytes=56 * 1024 * 1024
         ),
     )(
         q_start.T,
@@ -404,7 +453,7 @@
         ),
         in_specs=[vmem, vmem],
         out_specs=(vmem, vmem),
-    )(rows, product)
+    )(*(pltpu.with_memory_space_constraint(x, pltpu.VMEM) for x in (rows, product)))
     return basis_t.T, factor
 
 

time: 62.6 us -> 56.4 us (0.901)
  Pallas kernels: 61.7 us -> 55.7 us
    pallas_call x1, Pallas kernels: 60.1 us -> 54.9 us  [on_device(): pl.pallas_call(functools.partial(kernel, n_row, n_col, leaf * n_dev), nam...]
    pallas_call x1, Pallas kernels: 1.58 us -> 0.8 us  [on_device(): pl.pallas_call(finish, name='finish', out_shape=(jax.ShapeDtypeStruct((kc...]
where the time goes in v1:
time: 56.4 us; the launch traced here: 56.3 us
  Pallas kernels  55.7 us (99%)
  between operations  0.64 us (1%)
    pallas_call x1, Pallas kernels, on_device(): pl.pallas_call(functools.partial(kernel, n_row, n_col, leaf * n_dev), nam...  54.9 us

profile of v1, /device:TPU:0, one launch (start us, length us, event | category | flops | bytes accessed | tf_op | source)
XLA Modules:
  0.0 56.3 jit_solution(1339853521718080341)
XLA Ops:
  0.6 54.9 %subspace.1 = (f32[32,128]{1,0:T(8,128)S(1)}, f32[32,256]{1,0:T(8,128)S(1)}) custom-call(bf16[32,256]{1,0:T(8,128)(2,1)} %bitcast.14, f32[1,256]{1,0:T(1,128)} %bitcast.15, s32[128]{0:T(128)} %bitcast.16, s32[128]{0:T(128)} %bitcast.17, s32[128]{0:T(128)} %bitcast.18, s32[32]{0:T(128)} %bitcast.19, s32[32]{0:T(128)} %bitcast.20, ...), custom_call_target="tpu_custom_call" | custom-call | tf_op jit(solution)/shard_map/subspace/pallas_call | solution.py:395
  55.5 0.8 %finish.1 = (f32[32,256]{1,0:T(8,128)}, f32[32,32]{1,0:T(8,128)}) custom-call(f32[32,128]{1,0:T(8,128)S(1)} %get-tuple-element.6.rows_ref, f32[32,256]{1,0:T(8,128)S(1)} %get-tuple-element.7.prod_ref), custom_call_target="tpu_custom_call" | custom-call | tf_op jit(solution)/shard_map/finish/pallas_call | solution.py:447

commit v2 on v1

--- a/solution.py
+++ b/solution.py
@@ -121,6 +121,7 @@
     rs_ref,
     ga_ref,
     gb_ref,
+    gd_ref,
     load_sem,
     ag_send,
     ag_recv,
@@ -130,6 +131,7 @@
     ga_recv,
     gb_send,
     gb_recv,
+    gd_sem,
 ):
     row = lax.axis_index("row")
     col = lax.axis_index("col")
@@ -143,9 +145,7 @@
     low, high = lax.rem(row, pair), row // pair
     n_low, n_high = n_col * pair, n_row // pair
     peers = [(partner(row, d, n_row), col) for d in range(1, n_row)]
-    for e in range(pair):
-        for d in range(1, n_col):
-            peers.append((high * pair + lax.rem(low + e, pair), lax.rem(col + d, n_col)))
+    peers += [(row, partner(col, d, n_col)) for d in range(1, n_col)]
     barrier = pltpu.get_barrier_semaphore()
     for peer in peers:
         pl.semaphore_signal(barrier, inc=1, device_id=peer, device_id_type=MESH)
@@ -191,8 +191,8 @@
         wait_like(view, ag_recv.at[t])
 
     def scatter_start(t):
-        for d in range(n_col - 1, 0, -1):
-            peer = lax.rem(col + d, n_col)
+        for d in sorted(range(1, n_col), key=lambda d: (d % 2, -d)):
+            peer = partner(col, d, n_col)
             pltpu.make_async_remote_copy(
                 src_ref=out_ref.at[t, peer],
                 dst_ref=rs_ref.at[t, d - 1],
@@ -241,10 +241,31 @@
                 device_id_type=MESH,
             ).start()
 
+    def gram_all(value):
+        mine = row * n_col + col
+        gd_ref[mine] = value
+        for e in range(n_row - 1, -1, -1):
+            for d in range(n_col - 1, -1, -1):
+                if (d, e) == (0, 0):
+                    continue
+                pltpu.make_async_remote_copy(
+                    src_ref=gd_ref.at[mine],
+                    dst_ref=gd_ref.at[mine],
+                    send_sem=gd_sem.at[0],
+                    recv_sem=gd_sem.at[1],
+                    device_id=(partner(row, e, n_row), partner(col, d, n_col)),
+                    device_id_type=MESH,
+                ).start()
+        view = gd_ref.at[pl.ds(0, n_row * n_col - 1)]
+        wait_like(view, gd_sem.at[0])
+        wait_like(view, gd_sem.at[1])
+        return jnp.sum(gd_ref[...], axis=0)
+
     def gram_wait(t):
         view = gb_ref.at[t, pl.ds(0, n_high - 1)]
         wait_like(view, gb_send.at[t])
         wait_like(view, gb_recv.at[t])
+        return jnp.sum(gb_ref[t], axis=0)
 
     def selectors():
         place = lax.broadcasted_iota(jnp.int32, (SUB, TILE), 1)
@@ -265,9 +286,7 @@
 
         lax.fori_loop(0, far_tiles, tile, 0)
 
-    def operator(t, first):
-        if first:
-            loads[4].wait()
+    def operator(t):
         q_all = ag_refs[t][...].reshape(n_row * kcols, leaf)
 
         def far_tile(i, carry):
@@ -285,14 +304,9 @@
             return carry
 
         lax.fori_loop(0, far_tiles, far_tile, 0, unroll=True)
-        if first:
-            loads[5].wait()
         far = jnp.dot(lhs_ref[...], ut_ref[...], preferred_element_type=jnp.float32)
         for r in range(n_col):
             part_ref[t, r] = far[r * kcols : (r + 1) * kcols, :]
-        if first:
-            for i in (6, 7, 9):
-                loads[i].wait()
 
         def near_block(b, acc):
             z = dot_nt(ag_refs[t][nc_ref[b]], near_ref[b])
@@ -321,8 +335,8 @@
             packed = jnp.where(lane // kcols == i, g[i * rows : (i + 1) * rows, :], packed)
         return packed
 
-    def solve(t):
-        g = jnp.sum(gb_ref[t], axis=0) / total_pts
+    def solve(g):
+        g = g / total_pts
         parts = []
         for i in range(groups):
             shift = (1 - i) * kcols % LANES
@@ -332,23 +346,22 @@
         work = jnp.where(lane_full < 2 * kcols, work, 0.0)
         return factorize(work, kcols)
 
-    for i in (1, 2, 3):
-        loads[i].wait()
-    selectors()
     loads[0].wait()
     pl.semaphore_wait(barrier, len(peers))
     gather_start(0)
+    for copy in loads[1:4]:
+        copy.wait()
+    selectors()
+    for copy in loads[4:]:
+        copy.wait()
     for t in range(ITERS):
         if t > 0:
             gram_high_start(t - 1)
         gather_wait(t)
-        operator(t, t == 0)
+        operator(t)
         scatter_start(t)
         if t > 0:
-            gram_wait(t - 1)
-            rows = solve(t - 1)
-        if t == 0:
-            loads[8].wait()
+            rows = solve(gram_wait(t - 1))
         scatter_wait(t)
         total = part_ref[t, col]
         for d in range(1, n_col):
@@ -359,11 +372,9 @@
         if t < ITERS - 1:
             ag_refs[t + 1][row] = product.astype(jnp.bfloat16)
             gather_start(t + 1)
-        gram_low_start(t, pack_gram(product))
+            gram_low_start(t, pack_gram(product))
     prod_ref[...] = product
-    gram_high_start(ITERS - 1)
-    gram_wait(ITERS - 1)
-    rows_ref[...] = solve(ITERS - 1)
+    rows_ref[...] = solve(gram_all(pack_gram(product)))
 
 
 def on_device(
@@ -417,8 +428,9 @@
             pltpu.VMEM((ITERS, n_col, kcols, leaf), f32),
             pltpu.VMEM((ITERS, n_col, kcols, leaf), bf16),
             pltpu.VMEM((ITERS, n_col - 1, kcols, leaf), bf16),
-            pltpu.VMEM((ITERS, n_low, kcols * kcols // LANES, LANES), f32),
-            pltpu.VMEM((ITERS, n_high, kcols * kcols // LANES, LANES), f32),
+            pltpu.VMEM((ITERS - 1, n_low, kcols * kcols // LANES, LANES), f32),
+            pltpu.VMEM((ITERS - 1, n_high, kcols * kcols // LANES, LANES), f32),
+            pltpu.VMEM((n_dev, kcols * kcols // LANES, LANES), f32),
             pltpu.SemaphoreType.DMA((10,)),
             pltpu.SemaphoreType.DMA((ITERS,)),
             pltpu.SemaphoreType.DMA((ITERS,)),
@@ -428,6 +440,7 @@
             pltpu.SemaphoreType.DMA((ITERS,)),
             pltpu.SemaphoreType.DMA((ITERS,)),
             pltpu.SemaphoreType.DMA((ITERS,)),
+            pltpu.SemaphoreType.DMA((2,)),
         ],
         compiler_params=pltpu.CompilerParams(
             collective_id=0, has_side_effects=True, vmem_limit_bytes=56 * 1024 * 1024

time: 56.4 us -> 54.9 us (0.973)
  Pallas kernels: 55.7 us -> 54.1 us
    pallas_call x1, Pallas kernels: 54.9 us -> 53.3 us  [on_device(): pl.pallas_call(functools.partial(kernel, n_row, n_col, leaf * n_dev), nam...]
where the time goes in v2:
time: 54.9 us; the launch traced here: 54.7 us
  Pallas kernels  54.1 us (99%)
  between operations  0.64 us (1%)
    pallas_call x1, Pallas kernels, on_device(): pl.pallas_call(functools.partial(kernel, n_row, n_col, leaf * n_dev), nam...  53.3 us

profile of v2, /device:TPU:0, one launch (start us, length us, event | category | flops | bytes accessed | tf_op | source)
XLA Modules:
  0.0 54.7 jit_solution(9564182732047010058)
XLA Ops:
  0.6 53.3 %subspace.1 = (f32[32,128]{1,0:T(8,128)S(1)}, f32[32,256]{1,0:T(8,128)S(1)}) custom-call(bf16[32,256]{1,0:T(8,128)(2,1)} %bitcast.14, f32[1,256]{1,0:T(1,128)} %bitcast.15, s32[128]{0:T(128)} %bitcast.16, s32[128]{0:T(128)} %bitcast.17, s32[128]{0:T(128)} %bitcast.18, s32[32]{0:T(128)} %bitcast.19, s32[32]{0:T(128)} %bitcast.20, ...), custom_call_target="tpu_custom_call" | custom-call | tf_op jit(solution)/shard_map/subspace/pallas_call | solution.py:406
  53.9 0.8 %finish.1 = (f32[32,256]{1,0:T(8,128)}, f32[32,32]{1,0:T(8,128)}) custom-call(f32[32,128]{1,0:T(8,128)S(1)} %get-tuple-element.6.rows_ref, f32[32,256]{1,0:T(8,128)S(1)} %get-tuple-element.7.prod_ref), custom_call_target="tpu_custom_call" | custom-call | tf_op jit(solution)/shard_map/finish/pallas_call | solution.py:460

commit v3 on v2

--- a/solution.py
+++ b/solution.py
@@ -116,6 +116,7 @@
     ag_refs,
     sel_ref,
     lhs_ref,
+    vt_t_ref,
     part_ref,
     out_ref,
     rs_ref,
@@ -139,6 +140,7 @@
     groups = LANES // kcols
     far_tiles = ut_ref.shape[0] // TILE
     n_near = near_ref.shape[0]
+    n_parts = 4 if n_near % 4 == 0 else 1
     rank_max = ut_ref.shape[0] // rank_ref.shape[0]
 
     pair = 2 if n_row % 2 == 0 else 1
@@ -150,17 +152,19 @@
     for peer in peers:
         pl.semaphore_signal(barrier, inc=1, device_id=peer, device_id_type=MESH)
 
+    size = n_near // n_parts
+    parts = [pl.ds(i * size, size) for i in range(n_parts)]
     moves = (
         (q_hbm, ag_refs[0].at[row]),
         (rank_hbm, rank_ref),
         (fr_hbm, fr_ref),
         (fc_hbm, fc_ref),
-        (vt_hbm, vt_ref),
-        (ut_hbm, ut_ref),
         (nr_hbm, nr_ref),
         (nc_hbm, nc_ref),
         (scale_hbm, scale_ref),
-        (near_hbm, near_ref),
+        *((near_hbm.at[part], near_ref.at[part]) for part in parts),
+        (vt_hbm, vt_ref),
+        (ut_hbm, ut_ref),
     )
     loads = [
         pltpu.make_async_copy(src, dst, load_sem.at[i]) for i, (src, dst) in enumerate(moves)
@@ -289,36 +293,35 @@
     def operator(t):
         q_all = ag_refs[t][...].reshape(n_row * kcols, leaf)
 
-        def far_tile(i, carry):
-            start = pl.multiple_of(i * TILE, TILE)
-            y = dot_nt(q_all, vt_ref[pl.ds(start, TILE), :])
-            fc = jnp.concatenate([sel_ref[0, :, pl.ds(start, TILE)]] * (kcols // SUB), axis=0)
-            fr = jnp.concatenate([sel_ref[1, :, pl.ds(start, TILE)]] * (kcols // SUB), axis=0)
+        def far_tile(i):
+            tile = slice(i * TILE, (i + 1) * TILE)
+            y = jnp.dot(q_all, vt_t_ref[:, tile], preferred_element_type=jnp.float32)
+            fc = jnp.concatenate([sel_ref[0, :, tile]] * (kcols // SUB), axis=0)
+            fr = jnp.concatenate([sel_ref[1, :, tile]] * (kcols // SUB), axis=0)
             inner = jnp.zeros((kcols, TILE), jnp.float32)
             for c in range(n_row):
                 inner = jnp.where(fc == c, y[c * kcols : (c + 1) * kcols, :], inner)
             for r in range(n_col):
-                lhs_ref[r * kcols : (r + 1) * kcols, pl.ds(start, TILE)] = jnp.where(
+                lhs_ref[r * kcols : (r + 1) * kcols, tile] = jnp.where(
                     fr == r, inner, 0.0
                 ).astype(jnp.bfloat16)
-            return carry
-
-        lax.fori_loop(0, far_tiles, far_tile, 0, unroll=True)
+
+        def near_block(b, acc):
+            z = jnp.dot(ag_refs[t][nc_ref[b]], near_ref[b], preferred_element_type=jnp.float32)
+            r_of = nr_ref[b]
+            return [
+                a + z * jnp.where(r_of == r, 1.0, 0.0).astype(jnp.float32)
+                for r, a in enumerate(acc)
+            ]
+
+        near = [jnp.zeros((kcols, leaf), jnp.float32)] * n_col
+        for i in range(far_tiles):
+            far_tile(i)
+            for b in range(i * n_near // far_tiles, (i + 1) * n_near // far_tiles):
+                near = near_block(b, near)
         far = jnp.dot(lhs_ref[...], ut_ref[...], preferred_element_type=jnp.float32)
         for r in range(n_col):
-            part_ref[t, r] = far[r * kcols : (r + 1) * kcols, :]
-
-        def near_block(b, acc):
-            z = dot_nt(ag_refs[t][nc_ref[b]], near_ref[b])
-            r_of = nr_ref[b]
-            return tuple(
-                a + z * jnp.where(r_of == r, 1.0, 0.0).astype(jnp.float32) for r, a in enumerate(acc)
-            )
-
-        zero = jnp.zeros((kcols, leaf), jnp.float32)
-        near = lax.fori_loop(0, n_near, near_block, (zero,) * n_col, unroll=True)
-        for r in range(n_col):
-            whole = part_ref[t, r] + near[r]
+            whole = near[r] + far[r * kcols : (r + 1) * kcols, :]
             part_ref[t, r] = whole
             out_ref[t, r] = whole.astype(jnp.bfloat16)
 
@@ -352,7 +355,15 @@
     for copy in loads[1:4]:
         copy.wait()
     selectors()
-    for copy in loads[4:]:
+    for i in range(n_parts):
+        loads[7 + i].wait()
+        for b in range(i * size, (i + 1) * size):
+            near_ref[b] = near_ref[b].T
+    loads[7 + n_parts].wait()
+    for i in range(far_tiles):
+        tile = slice(i * TILE, (i + 1) * TILE)
+        vt_t_ref[:, tile] = vt_ref[tile, :].T
+    for copy in (*loads[4:7], loads[8 + n_parts]):
         copy.wait()
     for t in range(ITERS):
         if t > 0:
@@ -425,13 +436,14 @@
             [pltpu.VMEM((n_row, kcols, leaf), bf16) for _ in range(ITERS)],
             pltpu.VMEM((2, SUB, n_far * rank_max), jnp.int32),
             pltpu.VMEM((n_col * kcols, n_far * rank_max), bf16),
+            pltpu.VMEM((leaf, n_far * rank_max), bf16),
             pltpu.VMEM((ITERS, n_col, kcols, leaf), f32),
             pltpu.VMEM((ITERS, n_col, kcols, leaf), bf16),
             pltpu.VMEM((ITERS, n_col - 1, kcols, leaf), bf16),
             pltpu.VMEM((ITERS - 1, n_low, kcols * kcols // LANES, LANES), f32),
             pltpu.VMEM((ITERS - 1, n_high, kcols * kcols // LANES, LANES), f32),
             pltpu.VMEM((n_dev, kcols * kcols // LANES, LANES), f32),
-            pltpu.SemaphoreType.DMA((10,)),
+            pltpu.SemaphoreType.DMA((13,)),
             pltpu.SemaphoreType.DMA((ITERS,)),
             pltpu.SemaphoreType.DMA((ITERS,)),
             pltpu.SemaphoreType.DMA((ITERS,)),

time: 54.9 us -> 53.4 us (0.973)
  Pallas kernels: 54.1 us -> 52.6 us
    pallas_call x1, Pallas kernels: 53.3 us -> 51.8 us  [on_device(): pl.pallas_call(functools.partial(kernel, n_row, n_col, leaf * n_dev), nam...]
where the time goes in v3:
time: 53.4 us; the launch traced here: 53.2 us
  Pallas kernels  52.6 us (99%)
  between operations  0.64 us (1%)
    pallas_call x1, Pallas kernels, on_device(): pl.pallas_call(functools.partial(kernel, n_row, n_col, leaf * n_dev), nam...  51.8 us

profile of v3, /device:TPU:0, one launch (start us, length us, event | category | flops | bytes accessed | tf_op | source)
XLA Modules:
  0.0 53.2 jit_solution(3832733220862320398)
XLA Ops:
  0.6 51.8 %subspace.1 = (f32[32,128]{1,0:T(8,128)S(1)}, f32[32,256]{1,0:T(8,128)S(1)}) custom-call(bf16[32,256]{1,0:T(8,128)(2,1)} %bitcast.14, f32[1,256]{1,0:T(1,128)} %bitcast.15, s32[128]{0:T(128)} %bitcast.16, s32[128]{0:T(128)} %bitcast.17, s32[128]{0:T(128)} %bitcast.18, s32[32]{0:T(128)} %bitcast.19, s32[32]{0:T(128)} %bitcast.20, ...), custom_call_target="tpu_custom_call" | custom-call | tf_op jit(solution)/shard_map/subspace/pallas_call | solution.py:417
  52.4 0.8 %finish.1 = (f32[32,256]{1,0:T(8,128)}, f32[32,32]{1,0:T(8,128)}) custom-call(f32[32,128]{1,0:T(8,128)S(1)} %get-tuple-element.6.rows_ref, f32[32,256]{1,0:T(8,128)S(1)} %get-tuple-element.7.prod_ref), custom_call_target="tpu_custom_call" | custom-call | tf_op jit(solution)/shard_map/finish/pallas_call | solution.py:472

commit v4 on v3

--- a/solution.py
+++ b/solution.py
@@ -115,6 +115,7 @@
     vt_ref,
     ag_refs,
     sel_ref,
+    inner_ref,
     lhs_ref,
     vt_t_ref,
     part_ref,
@@ -138,7 +139,9 @@
     col = lax.axis_index("col")
     kcols, leaf = q_hbm.shape
     groups = LANES // kcols
+    half = n_row // 2 if n_row >= 4 and n_row & (n_row - 1) == 0 else n_row
     far_tiles = ut_ref.shape[0] // TILE
+    chunks = 4 if far_tiles % 4 == 0 else 1
     n_near = near_ref.shape[0]
     n_parts = 4 if n_near % 4 == 0 else 1
     rank_max = ut_ref.shape[0] // rank_ref.shape[0]
@@ -172,27 +175,29 @@
     for copy in loads:
         copy.start()
 
-    def ag_copy(t, peer):
+    def ag_copy(t, peer, late):
         return pltpu.make_async_remote_copy(
             src_ref=ag_refs[t].at[row],
             dst_ref=ag_refs[t].at[row],
-            send_sem=ag_send.at[t],
-            recv_sem=ag_recv.at[t],
+            send_sem=ag_send.at[t, late],
+            recv_sem=ag_recv.at[t, late],
             device_id=(peer, col),
             device_id_type=MESH,
         )
 
     def gather_start(t):
-        for d in range(n_row - 1, 0, -1):
-            ag_copy(t, partner(row, d, n_row)).start()
+        for d in sorted(range(1, n_row), key=lambda d: (d == 1, (d + 1) % 2, -d)):
+            ag_copy(t, partner(row, d, n_row), int(d >= half)).start()
 
     def wait_like(view, sem):
         pltpu.make_async_copy(view, view, sem).wait()
 
-    def gather_wait(t):
-        view = ag_refs[t].at[pl.ds(0, n_row - 1)]
-        wait_like(view, ag_send.at[t])
-        wait_like(view, ag_recv.at[t])
+    def gather_wait(t, late):
+        count = n_row - half if late else half - 1
+        if count:
+            view = ag_refs[t].at[pl.ds(0, count)]
+            wait_like(view, ag_send.at[t, late])
+            wait_like(view, ag_recv.at[t, late])
 
     def scatter_start(t):
         for d in sorted(range(1, n_col), key=lambda d: (d % 2, -d)):
@@ -290,17 +295,27 @@
 
         lax.fori_loop(0, far_tiles, tile, 0)
 
+    def far_inner(t, late, i):
+        first = lax.rem(row // half + late, n_row // half) * half
+        q_half = ag_refs[t][pl.ds(first, half)].reshape(half * kcols, leaf)
+        tile = slice(i * TILE, (i + 1) * TILE)
+        y = jnp.dot(q_half, vt_t_ref[:, tile], preferred_element_type=jnp.float32)
+        fc = jnp.concatenate([sel_ref[0, :, tile]] * (kcols // SUB), axis=0) - first
+        inner = inner_ref[:, tile] if late else jnp.zeros((kcols, TILE), jnp.float32)
+        for c in range(half):
+            inner = jnp.where(fc == c, y[c * kcols : (c + 1) * kcols, :], inner)
+        return inner
+
+    def far_early(t):
+        if half < n_row:
+            for i in range(far_tiles):
+                inner_ref[:, i * TILE : (i + 1) * TILE] = far_inner(t, 0, i)
+
     def operator(t):
-        q_all = ag_refs[t][...].reshape(n_row * kcols, leaf)
-
         def far_tile(i):
             tile = slice(i * TILE, (i + 1) * TILE)
-            y = jnp.dot(q_all, vt_t_ref[:, tile], preferred_element_type=jnp.float32)
-            fc = jnp.concatenate([sel_ref[0, :, tile]] * (kcols // SUB), axis=0)
+            inner = far_inner(t, int(half < n_row), i)
             fr = jnp.concatenate([sel_ref[1, :, tile]] * (kcols // SUB), axis=0)
-            inner = jnp.zeros((kcols, TILE), jnp.float32)
-            for c in range(n_row):
-                inner = jnp.where(fc == c, y[c * kcols : (c + 1) * kcols, :], inner)
             for r in range(n_col):
                 lhs_ref[r * kcols : (r + 1) * kcols, tile] = jnp.where(
                     fr == r, inner, 0.0
@@ -314,14 +329,27 @@
                 for r, a in enumerate(acc)
             ]
 
+        def far_chunk(g):
+            chunk = slice(g * far_tiles // chunks * TILE, (g + 1) * far_tiles // chunks * TILE)
+            far = jnp.dot(lhs_ref[:, chunk], ut_ref[chunk, :], preferred_element_type=jnp.float32)
+            for r in range(n_col):
+                piece = far[r * kcols : (r + 1) * kcols, :]
+                part_ref[t, r] = part_ref[t, r] + piece if g else piece
+
         near = [jnp.zeros((kcols, leaf), jnp.float32)] * n_col
+        done = 0
         for i in range(far_tiles):
             far_tile(i)
             for b in range(i * n_near // far_tiles, (i + 1) * n_near // far_tiles):
                 near = near_block(b, near)
-        far = jnp.dot(lhs_ref[...], ut_ref[...], preferred_element_type=jnp.float32)
+            if (done + 1) * far_tiles // chunks <= i + 1 - 1:
+                far_chunk(done)
+                done += 1
+        while done < chunks:
+            far_chunk(done)
+            done += 1
         for r in range(n_col):
-            whole = near[r] + far[r * kcols : (r + 1) * kcols, :]
+            whole = part_ref[t, r] + near[r]
             part_ref[t, r] = whole
             out_ref[t, r] = whole.astype(jnp.bfloat16)
 
@@ -348,6 +376,7 @@
         work = jnp.where(lane_full < kcols, jnp.where(lane_full == sub_full, 1.0, 0.0), s)
         work = jnp.where(lane_full < 2 * kcols, work, 0.0)
         return factorize(work, kcols)
+
 
     loads[0].wait()
     pl.semaphore_wait(barrier, len(peers))
@@ -368,7 +397,9 @@
     for t in range(ITERS):
         if t > 0:
             gram_high_start(t - 1)
-        gather_wait(t)
+        gather_wait(t, 0)
+        far_early(t)
+        gather_wait(t, 1)
         operator(t)
         scatter_start(t)
         if t > 0:
@@ -435,6 +466,7 @@
             pltpu.VMEM(vt.shape, bf16),
             [pltpu.VMEM((n_row, kcols, leaf), bf16) for _ in range(ITERS)],
             pltpu.VMEM((2, SUB, n_far * rank_max), jnp.int32),
+            pltpu.VMEM((kcols, n_far * rank_max), f32),
             pltpu.VMEM((n_col * kcols, n_far * rank_max), bf16),
             pltpu.VMEM((leaf, n_far * rank_max), bf16),
             pltpu.VMEM((ITERS, n_col, kcols, leaf), f32),
@@ -444,8 +476,8 @@
             pltpu.VMEM((ITERS - 1, n_high, kcols * kcols // LANES, LANES), f32),
             pltpu.VMEM((n_dev, kcols * kcols // LANES, LANES), f32),
             pltpu.SemaphoreType.DMA((13,)),
-            pltpu.SemaphoreType.DMA((ITERS,)),
-            pltpu.SemaphoreType.DMA((ITERS,)),
+            pltpu.SemaphoreType.DMA((ITERS, 2)),
+            pltpu.SemaphoreType.DMA((ITERS, 2)),
             pltpu.SemaphoreType.DMA((ITERS,)),
             pltpu.SemaphoreType.DMA((ITERS,)),
             pltpu.SemaphoreType.DMA((ITERS,)),

time: 53.4 us -> 51.4 us (0.963)
  Pallas kernels: 52.6 us -> 50.5 us
    pallas_call x1, Pallas kernels: 51.8 us -> 49.7 us  [on_device(): pl.pallas_call(functools.partial(kernel, n_row, n_col, leaf * n_dev), nam...]
where the time goes in v4:
time: 51.4 us; the launch traced here: 51.2 us
  Pallas kernels  50.5 us (98%)
  between operations  0.64 us (1%)
    pallas_call x1, Pallas kernels, on_device(): pl.pallas_call(functools.partial(kernel, n_row, n_col, leaf * n_dev), nam...  49.7 us

profile of v4, /device:TPU:0, one launch (start us, length us, event | category | flops | bytes accessed | tf_op | source)
XLA Modules:
  0.0 51.2 jit_solution(17879748023474285526)
XLA Ops:
  0.6 49.7 %subspace.1 = (f32[32,128]{1,0:T(8,128)S(1)}, f32[32,256]{1,0:T(8,128)S(1)}) custom-call(bf16[32,256]{1,0:T(8,128)(2,1)} %bitcast.14, f32[1,256]{1,0:T(1,128)} %bitcast.15, s32[128]{0:T(128)} %bitcast.16, s32[128]{0:T(128)} %bitcast.17, s32[128]{0:T(128)} %bitcast.18, s32[32]{0:T(128)} %bitcast.19, s32[32]{0:T(128)} %bitcast.20, ...), custom_call_target="tpu_custom_call" | custom-call | tf_op jit(solution)/shard_map/subspace/pallas_call | solution.py:448
  50.4 0.8 %finish.1 = (f32[32,256]{1,0:T(8,128)}, f32[32,32]{1,0:T(8,128)}) custom-call(f32[32,128]{1,0:T(8,128)S(1)} %get-tuple-element.6.rows_ref, f32[32,256]{1,0:T(8,128)S(1)} %get-tuple-element.7.prod_ref), custom_call_target="tpu_custom_call" | custom-call | tf_op jit(solution)/shard_map/finish/pallas_call | solution.py:504

commit v5 on v4

--- a/solution.py
+++ b/solution.py
@@ -219,8 +219,8 @@
     def gram_low_start(t, value):
         mine = low * n_col + col
         ga_ref[t, mine] = value
-        for e in range(pair - 1, -1, -1):
-            for d in range(n_col - 1, -1, -1):
+        for d in sorted(range(n_col), key=lambda d: (-(d // 2), d % 2)):
+            for e in range(pair - 1, -1, -1):
                 if (d, e) == (0, 0):
                     continue
                 pltpu.make_async_remote_copy(
@@ -230,7 +230,7 @@
                     recv_sem=ga_recv.at[t],
                     device_id=(
                         high * pair + lax.rem(low + e, pair),
-                        lax.rem(col + d, n_col),
+                        partner(col, d, n_col),
                     ),
                     device_id_type=MESH,
                 ).start()
@@ -253,8 +253,8 @@
     def gram_all(value):
         mine = row * n_col + col
         gd_ref[mine] = value
-        for e in range(n_row - 1, -1, -1):
-            for d in range(n_col - 1, -1, -1):
+        for d in sorted(range(n_col), key=lambda d: (-(d // 2), d % 2)):
+            for e in sorted(range(n_row), key=lambda e: (e < 2, (e + 1) % 2, -e)):
                 if (d, e) == (0, 0):
                     continue
                 pltpu.make_async_remote_copy(
@@ -338,9 +338,10 @@
 
         near = [jnp.zeros((kcols, leaf), jnp.float32)] * n_col
         done = 0
+        n_early = n_near // 2
         for i in range(far_tiles):
             far_tile(i)
-            for b in range(i * n_near // far_tiles, (i + 1) * n_near // far_tiles):
+            for b in range(i * n_early // far_tiles, (i + 1) * n_early // far_tiles):
                 near = near_block(b, near)
             if (done + 1) * far_tiles // chunks <= i + 1 - 1:
                 far_chunk(done)
@@ -348,6 +349,8 @@
         while done < chunks:
             far_chunk(done)
             done += 1
+        for b in range(n_early, n_near):
+            near = near_block(b, near)
         for r in range(n_col):
             whole = part_ref[t, r] + near[r]
             part_ref[t, r] = whole

time: 51.4 us -> 50 us (0.973)
  Pallas kernels: 50.5 us -> 49.1 us
    pallas_call x1, Pallas kernels: 49.7 us -> 48.3 us  [on_device(): pl.pallas_call(functools.partial(kernel, n_row, n_col, leaf * n_dev), nam...]
where the time goes in v5:
time: 50 us; the launch traced here: 49.8 us
  Pallas kernels  49.1 us (98%)
  between operations  0.64 us (1%)
    pallas_call x1, Pallas kernels, on_device(): pl.pallas_call(functools.partial(kernel, n_row, n_col, leaf * n_dev), nam...  48.3 us

profile of v5, /device:TPU:0, one launch (start us, length us, event | category | flops | bytes accessed | tf_op | source)
XLA Modules:
  0.0 49.8 jit_solution(15084138549923483919)
XLA Ops:
  0.6 48.3 %subspace.1 = (f32[32,128]{1,0:T(8,128)S(1)}, f32[32,256]{1,0:T(8,128)S(1)}) custom-call(bf16[32,256]{1,0:T(8,128)(2,1)} %bitcast.14, f32[1,256]{1,0:T(1,128)} %bitcast.15, s32[128]{0:T(128)} %bitcast.16, s32[128]{0:T(128)} %bitcast.17, s32[128]{0:T(128)} %bitcast.18, s32[32]{0:T(128)} %bitcast.19, s32[32]{0:T(128)} %bitcast.20, ...), custom_call_target="tpu_custom_call" | custom-call | tf_op jit(solution)/shard_map/subspace/pallas_call | solution.py:451
  49.0 0.8 %finish.1 = (f32[32,256]{1,0:T(8,128)}, f32[32,32]{1,0:T(8,128)}) custom-call(f32[32,128]{1,0:T(8,128)S(1)} %get-tuple-element.6.rows_ref, f32[32,256]{1,0:T(8,128)S(1)} %get-tuple-element.7.prod_ref), custom_call_target="tpu_custom_call" | custom-call | tf_op jit(solution)/shard_map/finish/pallas_call | solution.py:507

commit v6 on v5

--- a/solution.py
+++ b/solution.py
@@ -398,10 +398,10 @@
     for copy in (*loads[4:7], loads[8 + n_parts]):
         copy.wait()
     for t in range(ITERS):
+        gather_wait(t, 0)
+        far_early(t)
         if t > 0:
             gram_high_start(t - 1)
-        gather_wait(t, 0)
-        far_early(t)
         gather_wait(t, 1)
         operator(t)
         scatter_start(t)
@@ -483,10 +483,10 @@
             pltpu.SemaphoreType.DMA((ITERS, 2)),
             pltpu.SemaphoreType.DMA((ITERS,)),
             pltpu.SemaphoreType.DMA((ITERS,)),
-            pltpu.SemaphoreType.DMA((ITERS,)),
-            pltpu.SemaphoreType.DMA((ITERS,)),
-            pltpu.SemaphoreType.DMA((ITERS,)),
-            pltpu.SemaphoreType.DMA((ITERS,)),
+            pltpu.SemaphoreType.DMA((ITERS - 1,)),
+            pltpu.SemaphoreType.DMA((ITERS - 1,)),
+            pltpu.SemaphoreType.DMA((ITERS - 1,)),
+            pltpu.SemaphoreType.DMA((ITERS - 1,)),
             pltpu.SemaphoreType.DMA((2,)),
         ],
         compiler_params=pltpu.CompilerParams(

time: 50 us -> 50 us (level)
  no operation moved by 1% of the time
where the time goes in v6:
time: 50 us; the launch traced here: 49.8 us
  Pallas kernels  49.1 us (98%)
  between operations  0.64 us (1%)
    pallas_call x1, Pallas kernels, on_device(): pl.pallas_call(functools.partial(kernel, n_row, n_col, leaf * n_dev), nam...  48.3 us

profile of v6, /device:TPU:0, one launch (start us, length us, event | category | flops | bytes accessed | tf_op | source)
XLA Modules:
  0.0 49.8 jit_solution(1531727004979931558)
XLA Ops:
  0.6 48.3 %subspace.1 = (f32[32,128]{1,0:T(8,128)S(1)}, f32[32,256]{1,0:T(8,128)S(1)}) custom-call(bf16[32,256]{1,0:T(8,128)(2,1)} %bitcast.14, f32[1,256]{1,0:T(1,128)} %bitcast.15, s32[128]{0:T(128)} %bitcast.16, s32[128]{0:T(128)} %bitcast.17, s32[128]{0:T(128)} %bitcast.18, s32[32]{0:T(128)} %bitcast.19, s32[32]{0:T(128)} %bitcast.20, ...), custom_call_target="tpu_custom_call" | custom-call | tf_op jit(solution)/shard_map/subspace/pallas_call | solution.py:451
  49.0 0.8 %finish.1 = (f32[32,256]{1,0:T(8,128)}, f32[32,32]{1,0:T(8,128)}) custom-call(f32[32,128]{1,0:T(8,128)S(1)} %get-tuple-element.6.rows_ref, f32[32,256]{1,0:T(8,128)S(1)} %get-tuple-element.7.prod_ref), custom_call_target="tpu_custom_call" | custom-call | tf_op jit(solution)/shard_map/finish/pallas_call | solution.py:507
